TPU v7x, 32 devices: a whole 2x2x4 slice. The times are simulated.
32 devices in a mesh: cp: 16 (over z, y, x), hd: 2 (over core).
Axes of the slice: x: 2, y: 2, z: 4, core: 2. Of those that a mesh axis runs over, the one named last changes fastest.
Arguments:
- queries: bfloat16 [3072, 4096], P('cp', 'hd'), may hold values from -48 to 48
- keys: bfloat16 [3072, 1024], P('cp', 'hd'), may hold values from -48 to 48
- values: bfloat16 [3072, 1024], P('cp', 'hd'), may hold values from -6 to 6
- span_table: int32 [32], replicated, may hold values from 0 to 31, as said below
- doc_ids: int32 [3072], replicated, may hold values from 0 to 7, never falling along the last dimension, each value on 1 to 768 neighbouring positions
- out_weight: bfloat16 [4096, 4096], P('hd'), may hold values from -0.09375 to 0.09375
Outputs:
- mixed: bfloat16 [3072, 4096], P(('cp', 'hd'))
Inputs may be any that keep to these rules, and one draw needn't show every extreme that they name: `span_table`: slots 2 j and 2 j + 1 hold two spans c and 31 - c, and every span is held once.
All inputs are finite; a program needn't handle non-finite values.
Results may differ from a plain program's by a relative error of at most 0.0095.
Values may be sent and summed in bfloat16 or wider, within the bound.
A program may use at most 128 MiB of HBM per device.

v0:
```python
import jax
import jax.numpy as jnp
from jax import lax
from jax.sharding import PartitionSpec as P

HEAD_WIDTH = 128


def local(queries, keys, values, span_table, doc_ids, out_weight):
    tok_rows = queries.shape[0]
    span_len = tok_rows // 2
    span_count = span_table.shape[0]
    local_heads = queries.shape[1] // HEAD_WIDTH
    kv_heads = keys.shape[1] // HEAD_WIDTH
    query_group = local_heads // kv_heads
    scale = HEAD_WIDTH ** (-0.5)
    slot_onehot = (span_table[:, None] == jnp.arange(span_count, dtype=jnp.int32)[None, :]).astype(
        jnp.float32
    )
    doc_by_span = doc_ids.reshape(span_count, span_len).astype(jnp.float32)
    held_doc = jnp.dot(
        slot_onehot,
        doc_by_span,
        precision=lax.Precision.HIGHEST,
        preferred_element_type=jnp.float32,
    )
    held_doc = held_doc.astype(jnp.int32).reshape(span_count * span_len)
    held_pos = span_table[:, None] * span_len + jnp.arange(span_len, dtype=jnp.int32)[None, :]
    held_pos = held_pos.reshape(span_count * span_len)

    def locate(first):
        place = lax.dynamic_slice_in_dim(held_pos, first, tok_rows, 0)
        document = lax.dynamic_slice_in_dim(held_doc, first, tok_rows, 0)
        return (place, document)

    query_pos, query_doc = locate(lax.axis_index("cp") * tok_rows)
    query_heads = queries.reshape(tok_rows, kv_heads, query_group, HEAD_WIDTH)

    def visit(carry, key_block, value_block, key_start):
        key_pos, key_doc = locate(key_start)
        visible = (key_pos[None, :] <= query_pos[:, None]) & (
            key_doc[None, :] == query_doc[:, None]
        )

        def update(state):
            best, total, accum = state
            key_head_rows = key_block.reshape(tok_rows, kv_heads, HEAD_WIDTH)
            value_head_rows = value_block.reshape(tok_rows, kv_heads, HEAD_WIDTH)
            scores = (
                jnp.einsum(
                    "qkgd,nkd->kgqn", query_heads, key_head_rows, preferred_element_type=jnp.float32
                )
                * scale
            )
            scores = jnp.where(visible, scores, -1e30)
            new_best = jnp.maximum(best, jnp.max(scores, axis=-1))
            weights = jnp.where(visible, jnp.exp(scores - new_best[..., None]), 0.0)
            fade = jnp.exp(best - new_best)
            total = total * fade + jnp.sum(weights, axis=-1)
            accum = accum * fade[..., None] + jnp.einsum(
                "kgqn,nkd->kgqd",
                weights.astype(jnp.bfloat16),
                value_head_rows,
                preferred_element_type=jnp.float32,
            )
            return (new_best, total, accum)

        return lax.cond(jnp.any(visible), update, lambda state: state, carry)

    init = (
        jnp.full((kv_heads, query_group, tok_rows), -1e30, jnp.float32),
        jnp.zeros((kv_heads, query_group, tok_rows), jnp.float32),
        jnp.zeros((kv_heads, query_group, tok_rows, HEAD_WIDTH), jnp.float32),
    )
    key_piece = lax.all_gather(keys, "cp", axis=0, tiled=True)
    value_piece = lax.all_gather(values, "cp", axis=0, tiled=True)
    count = key_piece.shape[0] // tok_rows

    def step(index, state):
        offset = (index * tok_rows).astype(jnp.int32)
        key_block = lax.dynamic_slice_in_dim(key_piece, offset, tok_rows, 0)
        value_block = lax.dynamic_slice_in_dim(value_piece, offset, tok_rows, 0)
        return visit(state, key_block, value_block, offset)

    best, total, accum = lax.fori_loop(0, count, step, init)
    attn = (
        (accum / total[..., None])
        .transpose(2, 0, 1, 3)
        .reshape(tok_rows, local_heads * HEAD_WIDTH)
        .astype(jnp.bfloat16)
    )
    return lax.psum_scatter(
        jnp.dot(attn, out_weight, preferred_element_type=jnp.float32).astype(jnp.bfloat16),
        "hd",
        scatter_dimension=0,
        tiled=True,
    )


def solution(mesh):
    return jax.shard_map(
        local,
        mesh=mesh,
        in_specs=(P("cp", "hd"), P("cp", "hd"), P("cp", "hd"), P(), P(), P("hd", None)),
        out_specs=P(("cp", "hd"), None),
        check_vma=False,
    )
```

profile of v0, /device:TPU:0, one launch (start us, length us, event | category | flops | bytes accessed | tf_op | source)
XLA Modules:
  0.0 240.0 jit_solution(14145306607009826491)
XLA Ops:
  8.8 0.8 convolution_convert_fusion.1
  10.7 2.3 reshape.35
  13.2 67.5 %all-gather.3.cloned.1.call-done = bf16[3072,512]{1,0:T(8,128)(2,1)} async-done(((bf16[192,512]{1,0:T(8,128)(2,1)}), bf16[3072,512]{1,0:T(8,128)(2,1)}) %all-gather.3.cloned.1.call-update) | async-done | bytes 3145744 | tf_op jit(solution)/shard_map/all_gather | solution.py:75
  80.7 69.2 %all-gather.5.cloned.1.call-done = bf16[3072,512]{1,0:T(8,128)(2,1)} async-done(((bf16[192,512]{1,0:T(8,128)(2,1)}), bf16[3072,512]{1,0:T(8,128)(2,1)}) %all-gather.5.cloned.1.call-update) | async-done | bytes 3145744 | tf_op jit(solution)/shard_map/all_gather | solution.py:76
  150.1 59.1 %while.17 = (s32[]{:T(128)}, f32[4,4,192]{2,1,0:T(4,128)S(1)}, f32[4,4,192]{2,1,0:T(4,128)S(1)}, f32[4,4,192,128]{3,2,1,0:T(8,128)S(1)}, s32[3072]{0:T(1024)S(1)...) while((s32[]{:T(128)}, f32[4,4,192]{2,1,0:T(4,128)S(1)}, ...), condition=%wide.region_6.7_spmd, body=%wide.region_0.6_spmd.sunk | while | flops 310597632 | bytes 13326661 | solution.py:85
  150.3 0.7 fusion.26
  151.6 4.4 %conditional.2 = ((f32[4,4,192]{2,1,0:T(4,128)S(1)}, f32[4,4,192]{2,1,0:T(4,128)S(1)}, f32[4,4,192,128]{3,2,1,0:T(8,128)S(1)})) conditional(s32[]{:T(128)} %convert_element_type.51, (f32[4,4,192]{2,1,0:T(4,128)S(1)}, f32[4,4,192]{2,1,0:T(4,128)S(1)}, f32[4,4,192,128]{3,2,1,0:T(8,128)S(1)}) %tuple.49, (pred[192,192]{0,1:T(8,128)(4,1)S(1)}, ...), branch_computations={%region_2.0_spmd, %region_3.5_spmd} | conditional | flops 310450176 | bytes 13283364 | solution.py:68
  151.6 1.1 constant_dynamic-slice_fusion
  152.7 0.7 fusion
  153.5 0.8 fusion.2
  154.4 1.6 multiply_add_fusion
  157.5 4.4 %conditional.2 = ((f32[4,4,192]{2,1,0:T(4,128)S(1)}, f32[4,4,192]{2,1,0:T(4,128)S(1)}, f32[4,4,192,128]{3,2,1,0:T(8,128)S(1)})) conditional(s32[]{:T(128)} %convert_element_type.51, (f32[4,4,192]{2,1,0:T(4,128)S(1)}, f32[4,4,192]{2,1,0:T(4,128)S(1)}, f32[4,4,192,128]{3,2,1,0:T(8,128)S(1)}) %tuple.49, (pred[192,192]{0,1:T(8,128)(4,1)S(1)}, ...), branch_computations={%region_2.0_spmd, %region_3.5_spmd} | conditional | flops 310450176 | bytes 13283364 | solution.py:68
  157.5 1.1 constant_dynamic-slice_fusion
  158.7 0.7 fusion
  159.4 0.8 fusion.2
  160.3 1.6 multiply_add_fusion
  163.4 4.4 %conditional.2 = ((f32[4,4,192]{2,1,0:T(4,128)S(1)}, f32[4,4,192]{2,1,0:T(4,128)S(1)}, f32[4,4,192,128]{3,2,1,0:T(8,128)S(1)})) conditional(s32[]{:T(128)} %convert_element_type.51, (f32[4,4,192]{2,1,0:T(4,128)S(1)}, f32[4,4,192]{2,1,0:T(4,128)S(1)}, f32[4,4,192,128]{3,2,1,0:T(8,128)S(1)}) %tuple.49, (pred[192,192]{0,1:T(8,128)(4,1)S(1)}, ...), branch_computations={%region_2.0_spmd, %region_3.5_spmd} | conditional | flops 310450176 | bytes 13283364 | solution.py:68
  163.4 1.1 constant_dynamic-slice_fusion
  164.6 0.7 fusion
  165.3 0.8 fusion.2
  166.2 1.6 multiply_add_fusion
  173.7 4.4 %conditional.2 = ((f32[4,4,192]{2,1,0:T(4,128)S(1)}, f32[4,4,192]{2,1,0:T(4,128)S(1)}, f32[4,4,192,128]{3,2,1,0:T(8,128)S(1)})) conditional(s32[]{:T(128)} %convert_element_type.51, (f32[4,4,192]{2,1,0:T(4,128)S(1)}, f32[4,4,192]{2,1,0:T(4,128)S(1)}, f32[4,4,192,128]{3,2,1,0:T(8,128)S(1)}) %tuple.49, (pred[192,192]{0,1:T(8,128)(4,1)S(1)}, ...), branch_computations={%region_2.0_spmd, %region_3.5_spmd} | conditional | flops 310450176 | bytes 13283364 | solution.py:68
  173.8 1.1 constant_dynamic-slice_fusion
  174.9 0.7 fusion
  175.7 0.8 fusion.2
  176.5 1.6 multiply_add_fusion
  179.7 4.4 %conditional.2 = ((f32[4,4,192]{2,1,0:T(4,128)S(1)}, f32[4,4,192]{2,1,0:T(4,128)S(1)}, f32[4,4,192,128]{3,2,1,0:T(8,128)S(1)})) conditional(s32[]{:T(128)} %convert_element_type.51, (f32[4,4,192]{2,1,0:T(4,128)S(1)}, f32[4,4,192]{2,1,0:T(4,128)S(1)}, f32[4,4,192,128]{3,2,1,0:T(8,128)S(1)}) %tuple.49, (pred[192,192]{0,1:T(8,128)(4,1)S(1)}, ...), branch_computations={%region_2.0_spmd, %region_3.5_spmd} | conditional | flops 310450176 | bytes 13283364 | solution.py:68
  179.7 1.1 constant_dynamic-slice_fusion
  180.8 0.7 fusion
  181.6 0.8 fusion.2
  182.4 1.6 multiply_add_fusion
  185.6 4.4 %conditional.2 = ((f32[4,4,192]{2,1,0:T(4,128)S(1)}, f32[4,4,192]{2,1,0:T(4,128)S(1)}, f32[4,4,192,128]{3,2,1,0:T(8,128)S(1)})) conditional(s32[]{:T(128)} %convert_element_type.51, (f32[4,4,192]{2,1,0:T(4,128)S(1)}, f32[4,4,192]{2,1,0:T(4,128)S(1)}, f32[4,4,192,128]{3,2,1,0:T(8,128)S(1)}) %tuple.49, (pred[192,192]{0,1:T(8,128)(4,1)S(1)}, ...), branch_computations={%region_2.0_spmd, %region_3.5_spmd} | conditional | flops 310450176 | bytes 13283364 | solution.py:68
  185.6 1.1 constant_dynamic-slice_fusion
  186.7 0.7 fusion
  187.5 0.8 fusion.2
  188.4 1.6 multiply_add_fusion
  195.9 4.4 %conditional.2 = ((f32[4,4,192]{2,1,0:T(4,128)S(1)}, f32[4,4,192]{2,1,0:T(4,128)S(1)}, f32[4,4,192,128]{3,2,1,0:T(8,128)S(1)})) conditional(s32[]{:T(128)} %convert_element_type.51, (f32[4,4,192]{2,1,0:T(4,128)S(1)}, f32[4,4,192]{2,1,0:T(4,128)S(1)}, f32[4,4,192,128]{3,2,1,0:T(8,128)S(1)}) %tuple.49, (pred[192,192]{0,1:T(8,128)(4,1)S(1)}, ...), branch_computations={%region_2.0_spmd, %region_3.5_spmd} | conditional | flops 310450176 | bytes 13283364 | solution.py:68
  195.9 1.1 constant_dynamic-slice_fusion
  197.1 0.7 fusion
  197.9 0.8 fusion.2
  198.7 1.6 multiply_add_fusion
  201.8 4.4 %conditional.2 = ((f32[4,4,192]{2,1,0:T(4,128)S(1)}, f32[4,4,192]{2,1,0:T(4,128)S(1)}, f32[4,4,192,128]{3,2,1,0:T(8,128)S(1)})) conditional(s32[]{:T(128)} %convert_element_type.51, (f32[4,4,192]{2,1,0:T(4,128)S(1)}, f32[4,4,192]{2,1,0:T(4,128)S(1)}, f32[4,4,192,128]{3,2,1,0:T(8,128)S(1)}) %tuple.49, (pred[192,192]{0,1:T(8,128)(4,1)S(1)}, ...), branch_computations={%region_2.0_spmd, %region_3.5_spmd} | conditional | flops 310450176 | bytes 13283364 | solution.py:68
  201.8 1.1 constant_dynamic-slice_fusion
  203.0 0.7 fusion
  203.8 0.8 fusion.2
  204.6 1.6 multiply_add_fusion
  211.0 10.4 %convolution_convert_fusion = bf16[192,4096]{1,0:T(8,128)(2,1)} fusion(bf16[192,2048]{1,0:T(8,128)(2,1)S(1)} %convert_element_type.39, bf16[2048,4096]{1,0:T(8,128)(2,1)} %param.15), kind=kOutput, calls=%fused_computation.23 | convolution fusion | flops 3222011904 | bytes 19136512 | tf_op jit(solution)/shard_map/dot_general | solution.py:93
  221.3 12.2 %reduce-scatter.2.cloned.1.call-done = bf16[96,4096]{1,0:T(8,128)(2,1)} async-done(((bf16[192,4096]{1,0:T(8,128)(2,1)}), bf16[96,4096]{1,0:T(8,128)(2,1)}) %reduce-scatter.2.cloned.1.call-update) | async-done | bytes 786448 | tf_op jit(solution)/shard_map/reduce_scatter | solution.py:92
  (116 shorter events, 19.9 us)
Async XLA Ops:
  6.5 74.2 %all-gather.3.cloned.1.call-start = ((), (), s32[]{:S(2)}) async-start(), calls=%async_computation.1 | async-start | bytes 3342336 | tf_op jit(solution)/shard_map/all_gather | solution.py:75
  7.3 142.7 %all-gather.5.cloned.1.call-start = ((), (), s32[]{:S(2)}) async-start(), calls=%async_computation.2 | async-start | bytes 3342336 | tf_op jit(solution)/shard_map/all_gather | solution.py:76
  8.0 225.5 %reduce-scatter.2.cloned.1.call-start = ((), (), s32[]{:S(2)}) async-start(), calls=%async_computation.3 | async-start | bytes 2359296 | tf_op jit(solution)/shard_map/reduce_scatter | solution.py:92
Sparse Core Ops, SparseCore 0:
  10.1 70.5 all-gather.2
  83.5 66.3 all-gather.4
  221.5 11.9 reduce-scatter.1
where the time goes:
time: 241 us; the launch traced here: 240 us
  waiting for transfers between devices  150 us (62%)
  matrix products  30.1 us (12%)
  other arithmetic  20.4 us (8%)
  local copies, waits for them, and re-layouts  16 us (7%)
  between operations  13.2 us (5%)
  loops' own time  9.95 us (4%)
    all_gather x1, waiting for transfers between devices, local(): value_piece = lax.all_gather(values, 'cp', axis=0, tiled=True)  69.2 us
    all_gather x1, waiting for transfers between devices, local(): key_piece = lax.all_gather(keys, 'cp', axis=0, tiled=True)  67.5 us
    dot_general x8, matrix products, update(): jnp.einsum('kgqn,nkd->kgqd', weights.astype(jnp.bfloat16), value_head_row...  13.1 us
    reduce_scatter x1, waiting for transfers between devices, local(): lax.psum_scatter(jnp.dot(attn, out_weight, preferred_element_type=jnp.flo...  12.2 us
    reduce_or x16, other arithmetic, visit(): return lax.cond(jnp.any(visible), update, lambda state: state, carry)  11.6 us
    dot_general x1, matrix products, local(): jnp.dot(attn, out_weight, preferred_element_type=jnp.float32)  10.4 us
    another operation x1, loops' own time, local(): best, total, accum = lax.fori_loop(0, count, step, init)  9.39 us
    dynamic_slice x8, local copies, waits for them, and re-layouts, step(): value_block = lax.dynamic_slice_in_dim(value_piece, offset, tok_rows, 0)  8.44 us
  transfers between devices with their start and end apart: 3, of which 3 were waited for; matrix products, arithmetic and copies ran while one was open for 2% of the time, Pallas kernels for 0%

commit v1 on v0

--- a/solution.py
+++ b/solution.py
@@ -73,7 +73,12 @@
         jnp.zeros((kv_heads, query_group, tok_rows, HEAD_WIDTH), jnp.float32),
     )
     key_piece = lax.all_gather(keys, "cp", axis=0, tiled=True)
-    value_piece = lax.all_gather(values, "cp", axis=0, tiled=True)
+    ring = [values]
+    for hop in range(15):
+        ring.append(lax.ppermute(ring[-1], "cp", [(dev, (dev + 1) % 16) for dev in range(16)]))
+    value_piece = jnp.roll(
+        jnp.concatenate(ring[::-1], axis=0), (lax.axis_index("cp") + 1) * ring[0].shape[0], axis=0
+    )
     count = key_piece.shape[0] // tok_rows
 
     def step(index, state):

time: 241 us -> 360 us (1.49)
  local copies, waits for them, and re-layouts: 16 us -> 60.2 us
  other arithmetic: 20.4 us -> 55 us
  matrix products: 30.1 us -> 53.9 us
  waiting for transfers between devices: 150 us -> 160 us
    ppermute x0 -> x15, waiting for transfers between devices: none -> 148 us  [local(): lax.ppermute(ring[-1], 'cp', [(dev, (dev + 1) % 16) for dev in range(16)])]
    all_gather x1 -> x0, waiting for transfers between devices: 69.2 us -> none  [local(): value_piece = lax.all_gather(values, 'cp', axis=0, tiled=True)]
    all_gather x1, waiting for transfers between devices: 67.5 us -> 0.01 us  [local(): key_piece = lax.all_gather(keys, 'cp', axis=0, tiled=True)]
    reduce_or x16, other arithmetic: 11.6 us -> 33.8 us  [visit(): return lax.cond(jnp.any(visible), update, lambda state: state, carry)]
    dot_general x8, matrix products: 13.1 us -> 27.9 us  [update(): jnp.einsum('kgqn,nkd->kgqd', weights.astype(jnp.bfloat16), value_head_row...]
    dynamic_slice x17, local copies, waits for them, and re-layouts: 1.37 us -> 13.8 us  [locate(): document = lax.dynamic_slice_in_dim(held_doc, first, tok_rows, 0)]
    dynamic_slice x17, local copies, waits for them, and re-layouts: 1.28 us -> 13.5 us  [locate(): place = lax.dynamic_slice_in_dim(held_pos, first, tok_rows, 0)]
    cond x8 -> x72, local copies, waits for them, and re-layouts: 0.03 us -> 9.63 us
  transfers between devices with their start and end apart: 3 -> 17, of which waited for: 3 -> 16; matrix products, arithmetic and copies ran while one was open for 2% -> 5% of each run, Pallas kernels for 0% -> 0%
where the time goes in v1:
time: 360 us; the launch traced here: 357 us
  waiting for transfers between devices  160 us (44%)
  local copies, waits for them, and re-layouts  60.2 us (17%)
  other arithmetic  55 us (15%)
  matrix products  53.9 us (15%)
  between operations  13.7 us (4%)
  loops' own time  11.2 us (3%)
    ppermute x15, waiting for transfers between devices, local(): lax.ppermute(ring[-1], 'cp', [(dev, (dev + 1) % 16) for dev in range(16)])  148 us
    reduce_or x16, other arithmetic, visit(): return lax.cond(jnp.any(visible), update, lambda state: state, carry)  33.8 us
    dot_general x8, matrix products, update(): jnp.einsum('kgqn,nkd->kgqd', weights.astype(jnp.bfloat16), value_head_row...  27.9 us
    dot_general x8, matrix products, update(): jnp.einsum('qkgd,nkd->kgqn', query_heads, key_head_rows, preferred_elemen...  14.9 us
    dynamic_slice x17, local copies, waits for them, and re-layouts, locate(): document = lax.dynamic_slice_in_dim(held_doc, first, tok_rows, 0)  13.8 us
    dynamic_slice x17, local copies, waits for them, and re-layouts, locate(): place = lax.dynamic_slice_in_dim(held_pos, first, tok_rows, 0)  13.5 us
    reduce_sum x8, other arithmetic, update(): total = total * fade + jnp.sum(weights, axis=-1)  12.9 us
    reduce_scatter x1, waiting for transfers between devices, local(): lax.psum_scatter(jnp.dot(attn, out_weight, preferred_element_type=jnp.flo...  12.2 us
  transfers between devices with their start and end apart: 17, of which 16 were waited for; matrix products, arithmetic and copies ran while one was open for 5% of the time, Pallas kernels for 0%

profile of v1, /device:TPU:0, one launch (start us, length us, event | category | flops | bytes accessed | tf_op | source)
XLA Modules:
  0.0 357.3 jit_solution(17001830091705366998)
XLA Ops:
  6.5 3.0 collective-permute-start
  9.5 9.2 %collective-permute-done = bf16[192,512]{1,0:T(8,128)(2,1)S(1)} collective-permute-done((bf16[192,512]{1,0:T(8,128)(2,1)}, bf16[192,512]{1,0:T(8,128)(2,1)S(1)}, u32[]{:S(2)}, u32[]{:S(2)}) %collective-permute-start) | collective-permute-done | bytes 196640 | tf_op jit(solution)/shard_map/ppermute | solution.py:78
  18.7 9.7 %collective-permute-done.1 = bf16[192,512]{1,0:T(8,128)(2,1)S(1)} collective-permute-done((bf16[192,512]{1,0:T(8,128)(2,1)S(1)}, bf16[192,512]{1,0:T(8,128)(2,1)S(1)}, u32[]{:S(2)}, u32[]{:S(2)}) %collective-permute-start.1) | collective-permute-done | bytes 196640 | tf_op jit(solution)/shard_map/ppermute | solution.py:78
  28.3 9.3 %collective-permute-done.2 = bf16[192,512]{1,0:T(8,128)(2,1)S(1)} collective-permute-done((bf16[192,512]{1,0:T(8,128)(2,1)S(1)}, bf16[192,512]{1,0:T(8,128)(2,1)S(1)}, u32[]{:S(2)}, u32[]{:S(2)}) %collective-permute-start.2) | collective-permute-done | bytes 196640 | tf_op jit(solution)/shard_map/ppermute | solution.py:78
  37.6 9.3 %collective-permute-done.3 = bf16[192,512]{1,0:T(8,128)(2,1)S(1)} collective-permute-done((bf16[192,512]{1,0:T(8,128)(2,1)S(1)}, bf16[192,512]{1,0:T(8,128)(2,1)S(1)}, u32[]{:S(2)}, u32[]{:S(2)}) %collective-permute-start.3) | collective-permute-done | bytes 196640 | tf_op jit(solution)/shard_map/ppermute | solution.py:78
  46.9 9.3 %collective-permute-done.4 = bf16[192,512]{1,0:T(8,128)(2,1)S(1)} collective-permute-done((bf16[192,512]{1,0:T(8,128)(2,1)S(1)}, bf16[192,512]{1,0:T(8,128)(2,1)S(1)}, u32[]{:S(2)}, u32[]{:S(2)}) %collective-permute-start.4) | collective-permute-done | bytes 196640 | tf_op jit(solution)/shard_map/ppermute | solution.py:78
  56.1 9.3 %collective-permute-done.5 = bf16[192,512]{1,0:T(8,128)(2,1)S(1)} collective-permute-done((bf16[192,512]{1,0:T(8,128)(2,1)S(1)}, bf16[192,512]{1,0:T(8,128)(2,1)S(1)}, u32[]{:S(2)}, u32[]{:S(2)}) %collective-permute-start.5) | collective-permute-done | bytes 196640 | tf_op jit(solution)/shard_map/ppermute | solution.py:78
  65.5 10.3 %collective-permute-done.6 = bf16[192,512]{1,0:T(8,128)(2,1)S(1)} collective-permute-done((bf16[192,512]{1,0:T(8,128)(2,1)S(1)}, bf16[192,512]{1,0:T(8,128)(2,1)S(1)}, u32[]{:S(2)}, u32[]{:S(2)}) %collective-permute-start.6) | collective-permute-done | bytes 196640 | tf_op jit(solution)/shard_map/ppermute | solution.py:78
  75.8 14.2 %collective-permute-done.7 = bf16[192,512]{1,0:T(8,128)(2,1)S(1)} collective-permute-done((bf16[192,512]{1,0:T(8,128)(2,1)S(1)}, bf16[192,512]{1,0:T(8,128)(2,1)S(1)}, u32[]{:S(2)}, u32[]{:S(2)}) %collective-permute-start.7) | collective-permute-done | bytes 196640 | tf_op jit(solution)/shard_map/ppermute | solution.py:78
  90.0 11.6 %collective-permute-done.8 = bf16[192,512]{1,0:T(8,128)(2,1)S(1)} collective-permute-done((bf16[192,512]{1,0:T(8,128)(2,1)S(1)}, bf16[192,512]{1,0:T(8,128)(2,1)S(1)}, u32[]{:S(2)}, u32[]{:S(2)}) %collective-permute-start.8) | collective-permute-done | bytes 196640 | tf_op jit(solution)/shard_map/ppermute | solution.py:78
  101.7 11.8 %collective-permute-done.9 = bf16[192,512]{1,0:T(8,128)(2,1)S(1)} collective-permute-done((bf16[192,512]{1,0:T(8,128)(2,1)S(1)}, bf16[192,512]{1,0:T(8,128)(2,1)S(1)}, u32[]{:S(2)}, u32[]{:S(2)}) %collective-permute-start.9) | collective-permute-done | bytes 196640 | tf_op jit(solution)/shard_map/ppermute | solution.py:78
  113.4 11.2 %collective-permute-done.10 = bf16[192,512]{1,0:T(8,128)(2,1)S(1)} collective-permute-done((bf16[192,512]{1,0:T(8,128)(2,1)S(1)}, bf16[192,512]{1,0:T(8,128)(2,1)S(1)}, u32[]{:S(2)}, u32[]{:S(2)}) %collective-permute-start.10) | collective-permute-done | bytes 196640 | tf_op jit(solution)/shard_map/ppermute | solution.py:78
  125.4 13.8 %collective-permute-done.11 = bf16[192,512]{1,0:T(8,128)(2,1)S(1)} collective-permute-done((bf16[192,512]{1,0:T(8,128)(2,1)S(1)}, bf16[192,512]{1,0:T(8,128)(2,1)S(1)}, u32[]{:S(2)}, u32[]{:S(2)}) %collective-permute-start.11) | collective-permute-done | bytes 196640 | tf_op jit(solution)/shard_map/ppermute | solution.py:78
  140.8 7.7 %collective-permute-done.12 = bf16[192,512]{1,0:T(8,128)(2,1)S(1)} collective-permute-done((bf16[192,512]{1,0:T(8,128)(2,1)S(1)}, bf16[192,512]{1,0:T(8,128)(2,1)S(1)}, u32[]{:S(2)}, u32[]{:S(2)}) %collective-permute-start.12) | collective-permute-done | bytes 196640 | tf_op jit(solution)/shard_map/ppermute | solution.py:78
  149.1 8.7 %collective-permute-done.13 = bf16[192,512]{1,0:T(8,128)(2,1)} collective-permute-done((bf16[192,512]{1,0:T(8,128)(2,1)S(1)}, bf16[192,512]{1,0:T(8,128)(2,1)}, u32[]{:S(2)}, u32[]{:S(2)}) %collective-permute-start.13) | collective-permute-done | bytes 196640 | tf_op jit(solution)/shard_map/ppermute | solution.py:78
  161.3 2.3 reshape.35
  164.7 2.7 collective-permute-done.14
  171.9 2.5 constant_dynamic-slice_fusion.2
  175.7 149.1 %while.17 = (s32[]{:T(128)}, f32[4,4,192]{2,1,0:T(4,128)S(1)}, f32[4,4,192]{2,1,0:T(4,128)S(1)}, f32[4,4,192,128]{3,2,1,0:T(8,128)}, s32[3072]{0:T(1024)}, /*ind...) while((s32[]{:T(128)}, f32[4,4,192]{2,1,0:T(4,128)S(1)}, ...), condition=%wide.region_6.7_spmd, body=%wide.region_0.6_spmd.sunk | while | flops 310597632 | bytes 13523381 | solution.py:90
  177.2 2.1 fusion.26
  179.9 10.0 %conditional.2 = ((f32[4,4,192]{2,1,0:T(4,128)S(1)}, f32[4,4,192]{2,1,0:T(4,128)S(1)}, f32[4,4,192,128]{3,2,1,0:T(8,128)})) conditional(s32[]{:T(128)} %convert_element_type.51, (f32[4,4,192]{2,1,0:T(4,128)S(1)}, f32[4,4,192]{2,1,0:T(4,128)S(1)}, f32[4,4,192,128]{3,2,1,0:T(8,128)}) %tuple.49, (pred[192,192]{0,1:T(8,128)(4,1)}, ...), branch_computations={%region_2.2_spmd, %region_3.5_spmd} | conditional | flops 310450176 | bytes 13480084 | solution.py:68
  186.5 3.5 multiply_add_fusion
  194.3 10.0 %conditional.2 = ((f32[4,4,192]{2,1,0:T(4,128)S(1)}, f32[4,4,192]{2,1,0:T(4,128)S(1)}, f32[4,4,192,128]{3,2,1,0:T(8,128)})) conditional(s32[]{:T(128)} %convert_element_type.51, (f32[4,4,192]{2,1,0:T(4,128)S(1)}, f32[4,4,192]{2,1,0:T(4,128)S(1)}, f32[4,4,192,128]{3,2,1,0:T(8,128)}) %tuple.49, (pred[192,192]{0,1:T(8,128)(4,1)}, ...), branch_computations={%region_2.2_spmd, %region_3.5_spmd} | conditional | flops 310450176 | bytes 13480084 | solution.py:68
  200.8 3.5 multiply_add_fusion
  205.9 2.1 fusion.26
  208.6 10.0 %conditional.2 = ((f32[4,4,192]{2,1,0:T(4,128)S(1)}, f32[4,4,192]{2,1,0:T(4,128)S(1)}, f32[4,4,192,128]{3,2,1,0:T(8,128)})) conditional(s32[]{:T(128)} %convert_element_type.51, (f32[4,4,192]{2,1,0:T(4,128)S(1)}, f32[4,4,192]{2,1,0:T(4,128)S(1)}, f32[4,4,192,128]{3,2,1,0:T(8,128)}) %tuple.49, (pred[192,192]{0,1:T(8,128)(4,1)}, ...), branch_computations={%region_2.2_spmd, %region_3.5_spmd} | conditional | flops 310450176 | bytes 13480084 | solution.py:68
  215.1 3.5 multiply_add_fusion
  224.5 2.1 fusion.26
  228.8 2.1 fusion.26
  235.9 10.0 %conditional.2 = ((f32[4,4,192]{2,1,0:T(4,128)S(1)}, f32[4,4,192]{2,1,0:T(4,128)S(1)}, f32[4,4,192,128]{3,2,1,0:T(8,128)})) conditional(s32[]{:T(128)} %convert_element_type.51, (f32[4,4,192]{2,1,0:T(4,128)S(1)}, f32[4,4,192]{2,1,0:T(4,128)S(1)}, f32[4,4,192,128]{3,2,1,0:T(8,128)}) %tuple.49, (pred[192,192]{0,1:T(8,128)(4,1)}, ...), branch_computations={%region_2.2_spmd, %region_3.5_spmd} | conditional | flops 310450176 | bytes 13480084 | solution.py:68
  242.4 3.5 multiply_add_fusion
  247.5 2.1 fusion.26
  250.3 10.0 %conditional.2 = ((f32[4,4,192]{2,1,0:T(4,128)S(1)}, f32[4,4,192]{2,1,0:T(4,128)S(1)}, f32[4,4,192,128]{3,2,1,0:T(8,128)})) conditional(s32[]{:T(128)} %convert_element_type.51, (f32[4,4,192]{2,1,0:T(4,128)S(1)}, f32[4,4,192]{2,1,0:T(4,128)S(1)}, f32[4,4,192,128]{3,2,1,0:T(8,128)}) %tuple.49, (pred[192,192]{0,1:T(8,128)(4,1)}, ...), branch_computations={%region_2.2_spmd, %region_3.5_spmd} | conditional | flops 310450176 | bytes 13480084 | solution.py:68
  256.8 3.5 multiply_add_fusion
  261.9 2.1 fusion.26
  264.6 10.0 %conditional.2 = ((f32[4,4,192]{2,1,0:T(4,128)S(1)}, f32[4,4,192]{2,1,0:T(4,128)S(1)}, f32[4,4,192,128]{3,2,1,0:T(8,128)})) conditional(s32[]{:T(128)} %convert_element_type.51, (f32[4,4,192]{2,1,0:T(4,128)S(1)}, f32[4,4,192]{2,1,0:T(4,128)S(1)}, f32[4,4,192,128]{3,2,1,0:T(8,128)}) %tuple.49, (pred[192,192]{0,1:T(8,128)(4,1)}, ...), branch_computations={%region_2.2_spmd, %region_3.5_spmd} | conditional | flops 310450176 | bytes 13480084 | solution.py:68
  271.1 3.5 multiply_add_fusion
  276.2 2.1 fusion.26
  284.9 2.1 fusion.26
  291.9 10.0 %conditional.2 = ((f32[4,4,192]{2,1,0:T(4,128)S(1)}, f32[4,4,192]{2,1,0:T(4,128)S(1)}, f32[4,4,192,128]{3,2,1,0:T(8,128)})) conditional(s32[]{:T(128)} %convert_element_type.51, (f32[4,4,192]{2,1,0:T(4,128)S(1)}, f32[4,4,192]{2,1,0:T(4,128)S(1)}, f32[4,4,192,128]{3,2,1,0:T(8,128)}) %tuple.49, (pred[192,192]{0,1:T(8,128)(4,1)}, ...), branch_computations={%region_2.2_spmd, %region_3.5_spmd} | conditional | flops 310450176 | bytes 13480084 | solution.py:68
  298.4 3.5 multiply_add_fusion
  303.4 2.1 fusion.26
  306.2 10.0 %conditional.2 = ((f32[4,4,192]{2,1,0:T(4,128)S(1)}, f32[4,4,192]{2,1,0:T(4,128)S(1)}, f32[4,4,192,128]{3,2,1,0:T(8,128)})) conditional(s32[]{:T(128)} %convert_element_type.51, (f32[4,4,192]{2,1,0:T(4,128)S(1)}, f32[4,4,192]{2,1,0:T(4,128)S(1)}, f32[4,4,192,128]{3,2,1,0:T(8,128)}) %tuple.49, (pred[192,192]{0,1:T(8,128)(4,1)}, ...), branch_computations={%region_2.2_spmd, %region_3.5_spmd} | conditional | flops 310450176 | bytes 13480084 | solution.py:68
  312.7 3.5 multiply_add_fusion
  317.7 2.1 fusion.26
  322.0 2.1 fusion.26
  327.9 10.4 %convolution_convert_fusion = bf16[192,4096]{1,0:T(8,128)(2,1)} fusion(bf16[192,2048]{1,0:T(8,128)(2,1)S(1)} %convert_element_type.39, bf16[2048,4096]{1,0:T(8,128)(2,1)} %param.15), kind=kOutput, calls=%fused_computation.23 | convolution fusion | flops 3222011904 | bytes 19136512 | tf_op jit(solution)/shard_map/dot_general | solution.py:98
  338.2 12.2 %reduce-scatter.2.cloned.1.call-done = bf16[96,4096]{1,0:T(8,128)(2,1)} async-done(((bf16[192,4096]{1,0:T(8,128)(2,1)}), bf16[96,4096]{1,0:T(8,128)(2,1)}) %reduce-scatter.2.cloned.1.call-update) | async-done | bytes 786448 | tf_op jit(solution)/shard_map/reduce_scatter | solution.py:97
  (242 shorter events, 103.1 us)
Async XLA Ops:
  6.5 163.1 %copy-start.4 = (bf16[192,512]{1,0:T(8,128)(2,1)S(1)}, bf16[192,512]{1,0:T(8,128)(2,1)}, u32[]{:S(2)}) copy-start(bf16[192,512]{1,0:T(8,128)(2,1)} %param.12) | copy-start | bytes 589828
  6.5 167.8 %all-gather.2.cloned.1.call-start = ((), (), s32[]{:S(2)}) async-start(), calls=%async_computation.1 | async-start | bytes 3342336 | tf_op jit(solution)/shard_map/all_gather | solution.py:75
  6.5 12.1 %collective-permute-start = (bf16[192,512]{1,0:T(8,128)(2,1)}, bf16[192,512]{1,0:T(8,128)(2,1)S(1)}, u32[]{:S(2)}, u32[]{:S(2)}) collective-permute-start(bf16[192,512]{1,0:T(8,128)(2,1)} %param.12), channel_id=1, source_target_pairs={{0,2},{2,4},{4,6},{6,8},{8,10},{10,12},{12,14},{14,16},{16,18},{18... | collective-permute-start | bytes 589832 | tf_op jit(solution)/shard_map/ppermute | solution.py:78
  18.7 9.7 %collective-permute-start.1 = (bf16[192,512]{1,0:T(8,128)(2,1)S(1)}, bf16[192,512]{1,0:T(8,128)(2,1)S(1)}, u32[]{:S(2)}, u32[]{:S(2)}) collective-permute-start(bf16[192,512]{1,0:T(8,128)(2,1)S(1)} %collective-permute-done), channel_id=1, source_target_pairs={{0,2},{2,4},{4,6},{6,8},{8,10},{10,12},{12,14},{14,16},{16,18},{18... | collective-permute-start | bytes 589832 | tf_op jit(solution)/shard_map/ppermute | solution.py:78
  28.3 9.3 %collective-permute-start.2 = (bf16[192,512]{1,0:T(8,128)(2,1)S(1)}, bf16[192,512]{1,0:T(8,128)(2,1)S(1)}, u32[]{:S(2)}, u32[]{:S(2)}) collective-permute-start(bf16[192,512]{1,0:T(8,128)(2,1)S(1)} %collective-permute-done.1), channel_id=1, source_target_pairs={{0,2},{2,4},{4,6},{6,8},{8,10},{10,12},{12,14},{14,16},{16,18},{18... | collective-permute-start | bytes 589832 | tf_op jit(solution)/shard_map/ppermute | solution.py:78
  37.6 9.3 %collective-permute-start.3 = (bf16[192,512]{1,0:T(8,128)(2,1)S(1)}, bf16[192,512]{1,0:T(8,128)(2,1)S(1)}, u32[]{:S(2)}, u32[]{:S(2)}) collective-permute-start(bf16[192,512]{1,0:T(8,128)(2,1)S(1)} %collective-permute-done.2), channel_id=1, source_target_pairs={{0,2},{2,4},{4,6},{6,8},{8,10},{10,12},{12,14},{14,16},{16,18},{18... | collective-permute-start | bytes 589832 | tf_op jit(solution)/shard_map/ppermute | solution.py:78
  46.9 9.3 %collective-permute-start.4 = (bf16[192,512]{1,0:T(8,128)(2,1)S(1)}, bf16[192,512]{1,0:T(8,128)(2,1)S(1)}, u32[]{:S(2)}, u32[]{:S(2)}) collective-permute-start(bf16[192,512]{1,0:T(8,128)(2,1)S(1)} %collective-permute-done.3), channel_id=1, source_target_pairs={{0,2},{2,4},{4,6},{6,8},{8,10},{10,12},{12,14},{14,16},{16,18},{18... | collective-permute-start | bytes 589832 | tf_op jit(solution)/shard_map/ppermute | solution.py:78
  56.1 9.3 %collective-permute-start.5 = (bf16[192,512]{1,0:T(8,128)(2,1)S(1)}, bf16[192,512]{1,0:T(8,128)(2,1)S(1)}, u32[]{:S(2)}, u32[]{:S(2)}) collective-permute-start(bf16[192,512]{1,0:T(8,128)(2,1)S(1)} %collective-permute-done.4), channel_id=1, source_target_pairs={{0,2},{2,4},{4,6},{6,8},{8,10},{10,12},{12,14},{14,16},{16,18},{18... | collective-permute-start | bytes 589832 | tf_op jit(solution)/shard_map/ppermute | solution.py:78
  65.4 10.4 %collective-permute-start.6 = (bf16[192,512]{1,0:T(8,128)(2,1)S(1)}, bf16[192,512]{1,0:T(8,128)(2,1)S(1)}, u32[]{:S(2)}, u32[]{:S(2)}) collective-permute-start(bf16[192,512]{1,0:T(8,128)(2,1)S(1)} %collective-permute-done.5), channel_id=1, source_target_pairs={{0,2},{2,4},{4,6},{6,8},{8,10},{10,12},{12,14},{14,16},{16,18},{18... | collective-permute-start | bytes 589832 | tf_op jit(solution)/shard_map/ppermute | solution.py:78
  65.4 285.0 %reduce-scatter.2.cloned.1.call-start = ((), (), s32[]{:S(2)}) async-start(), calls=%async_computation.2 | async-start | bytes 2359296 | tf_op jit(solution)/shard_map/reduce_scatter | solution.py:97
  75.8 14.2 %collective-permute-start.7 = (bf16[192,512]{1,0:T(8,128)(2,1)S(1)}, bf16[192,512]{1,0:T(8,128)(2,1)S(1)}, u32[]{:S(2)}, u32[]{:S(2)}) collective-permute-start(bf16[192,512]{1,0:T(8,128)(2,1)S(1)} %collective-permute-done.6), channel_id=1, source_target_pairs={{0,2},{2,4},{4,6},{6,8},{8,10},{10,12},{12,14},{14,16},{16,18},{18... | collective-permute-start | bytes 589832 | tf_op jit(solution)/shard_map/ppermute | solution.py:78
  90.0 11.6 %collective-permute-start.8 = (bf16[192,512]{1,0:T(8,128)(2,1)S(1)}, bf16[192,512]{1,0:T(8,128)(2,1)S(1)}, u32[]{:S(2)}, u32[]{:S(2)}) collective-permute-start(bf16[192,512]{1,0:T(8,128)(2,1)S(1)} %collective-permute-done.7), channel_id=1, source_target_pairs={{0,2},{2,4},{4,6},{6,8},{8,10},{10,12},{12,14},{14,16},{16,18},{18... | collective-permute-start | bytes 589832 | tf_op jit(solution)/shard_map/ppermute | solution.py:78
  101.6 11.8 %collective-permute-start.9 = (bf16[192,512]{1,0:T(8,128)(2,1)S(1)}, bf16[192,512]{1,0:T(8,128)(2,1)S(1)}, u32[]{:S(2)}, u32[]{:S(2)}) collective-permute-start(bf16[192,512]{1,0:T(8,128)(2,1)S(1)} %collective-permute-done.8), channel_id=1, source_target_pairs={{0,2},{2,4},{4,6},{6,8},{8,10},{10,12},{12,14},{14,16},{16,18},{18... | collective-permute-start | bytes 589832 | tf_op jit(solution)/shard_map/ppermute | solution.py:78
  113.4 11.2 %collective-permute-start.10 = (bf16[192,512]{1,0:T(8,128)(2,1)S(1)}, bf16[192,512]{1,0:T(8,128)(2,1)S(1)}, u32[]{:S(2)}, u32[]{:S(2)}) collective-permute-start(bf16[192,512]{1,0:T(8,128)(2,1)S(1)} %collective-permute-done.9), channel_id=1, source_target_pairs={{0,2},{2,4},{4,6},{6,8},{8,10},{10,12},{12,14},{14,16},{16,18},{18... | collective-permute-start | bytes 589832 | tf_op jit(solution)/shard_map/ppermute | solution.py:78
  124.6 14.6 %collective-permute-start.11 = (bf16[192,512]{1,0:T(8,128)(2,1)S(1)}, bf16[192,512]{1,0:T(8,128)(2,1)S(1)}, u32[]{:S(2)}, u32[]{:S(2)}) collective-permute-start(bf16[192,512]{1,0:T(8,128)(2,1)S(1)} %collective-permute-done.10), channel_id=1, source_target_pairs={{0,2},{2,4},{4,6},{6,8},{8,10},{10,12},{12,14},{14,16},{16,18},{18... | collective-permute-start | bytes 589832 | tf_op jit(solution)/shard_map/ppermute | solution.py:78
  139.2 9.3 %collective-permute-start.12 = (bf16[192,512]{1,0:T(8,128)(2,1)S(1)}, bf16[192,512]{1,0:T(8,128)(2,1)S(1)}, u32[]{:S(2)}, u32[]{:S(2)}) collective-permute-start(bf16[192,512]{1,0:T(8,128)(2,1)S(1)} %collective-permute-done.11), channel_id=1, source_target_pairs={{0,2},{2,4},{4,6},{6,8},{8,10},{10,12},{12,14},{14,16},{16,18},{18... | collective-permute-start | bytes 589832 | tf_op jit(solution)/shard_map/ppermute | solution.py:78
  148.5 9.4 %collective-permute-start.13 = (bf16[192,512]{1,0:T(8,128)(2,1)S(1)}, bf16[192,512]{1,0:T(8,128)(2,1)}, u32[]{:S(2)}, u32[]{:S(2)}) collective-permute-start(bf16[192,512]{1,0:T(8,128)(2,1)S(1)} %collective-permute-done.12), channel_id=1, source_target_pairs={{0,2},{2,4},{4,6},{6,8},{8,10},{10,12},{12,14},{14,16},{16,18},{18... | collective-permute-start | bytes 589832 | tf_op jit(solution)/shard_map/ppermute | solution.py:78
  157.8 9.6 %collective-permute-start.14 = (bf16[192,512]{1,0:T(8,128)(2,1)}, bf16[192,512]{1,0:T(8,128)(2,1)}, u32[]{:S(2)}, u32[]{:S(2)}) collective-permute-start(bf16[192,512]{1,0:T(8,128)(2,1)} %collective-permute-done.13), channel_id=1, source_target_pairs={{0,2},{2,4},{4,6},{6,8},{8,10},{10,12},{12,14},{14,16},{16,18},{18... | collective-permute-start | bytes 589832 | tf_op jit(solution)/shard_map/ppermute | solution.py:78
  180.0 0.6 copy-start
  181.7 3.5 copy-start.1
  185.8 0.6 copy-start.2
  186.5 3.5 copy-start.3
  194.3 0.6 copy-start
  196.0 3.5 copy-start.1
  200.1 0.6 copy-start.2
  200.8 3.5 copy-start.3
  208.6 0.6 copy-start
  210.3 3.5 copy-start.1
  214.5 0.6 copy-start.2
  215.1 3.5 copy-start.3
  235.9 0.6 copy-start
  237.6 3.5 copy-start.1
  241.8 0.6 copy-start.2
  242.4 3.5 copy-start.3
  250.3 0.6 copy-start
  252.0 3.5 copy-start.1
  256.1 0.6 copy-start.2
  256.8 3.5 copy-start.3
  264.6 0.6 copy-start
  266.3 3.5 copy-start.1
  271.1 3.5 copy-start.3
  291.9 0.6 copy-start
  293.6 3.5 copy-start.1
  298.4 3.5 copy-start.3
  306.2 0.6 copy-start
  307.9 3.5 copy-start.1
  312.0 0.6 copy-start.2
  312.7 3.5 copy-start.3
  (2 other events, 1.2 us)
Sparse Core Ops, SparseCore 0:
  65.6 78.8 all-gather.1
  338.4 12.0 reduce-scatter.1
